TPU v7x, 32 devices: a whole 2x2x4 slice. The times are simulated.
32 devices in a mesh: seq: 8 (over z, x), head: 4 (over y, core).
Axes of the slice: x: 2, y: 2, z: 4, core: 2. Of those that a mesh axis runs over, the one named last changes fastest.
Arguments:
- queries: bfloat16 [8192, 2048], P('seq', 'head'), may hold values from -64 to 64
- keys: bfloat16 [8192, 2048], P('seq', 'head'), may hold values from -16 to 16
- values: bfloat16 [8192, 2048], P('seq', 'head'), may hold values from -6 to 6
- span_bounds: int32 [16, 2], replicated, may hold values from 0 to 8192, as said below
- mem_decay: float32 [8, 16], P(None, 'head'), may hold values from 0.01 to 1
- mem_gate: float32 [16], P('head'), may hold values from -2 to 2
- out_weight: bfloat16 [2048, 4096], P('head'), may hold values from -0.125 to 0.125
Outputs:
- mixed: bfloat16 [8192, 4096], P('seq', 'head')
Inputs may be any that keep to these rules, and one draw needn't show every extreme that they name: `span_bounds`: slot k lies in segment k // 2, inside the k % 2-th of 2 equal parts of it; start <= end, an empty slot has start == end; some slot covers a whole part.
All inputs are finite; a program needn't handle non-finite values.
Results may differ from a plain program's by a relative error of at most 0.0052.
The roundings to bfloat16 on the way count: a program that leaves them out, or rounds other values in their place, can miss the bound.
Values may be sent and summed in bfloat16 or wider, within the bound.
No kernel may reach another device: no remote copies, remote signals or barrier semaphores. Data moves between devices by JAX's collectives and lax.ppermute only.
A program may use at most 128 MiB of HBM per device.

v0:
```python
import math
import jax
import jax.numpy as jnp
from jax import lax
from jax.sharding import PartitionSpec as P

BAND = 512
SPAN_DEV = 2
HIGHEST_PRECISION = lax.Precision.HIGHEST


def from_behind(block, axis, distance):
    devices = range(lax.axis_size(axis))
    route = [(i - distance, i) for i in devices if i - distance in devices]
    return lax.ppermute(block, axis, route)


def feature_map(values_in):
    return jnp.where(values_in > 0, values_in + 1.0, jnp.exp(jnp.minimum(values_in, 0.0)))


def local_attention(
    queries_3d, band_keys, band_values, query_labels, key_labels, shard_index, band_width
):
    seg_rows, head_count, head_width = queries_3d.shape
    block_rows = min(seg_rows, 512)
    key_count = band_keys.shape[0]
    key_pos = jnp.arange(key_count) - band_width
    key_valid = (key_pos >= 0) | (shard_index > 0)
    score_scale = 1.0 / math.sqrt(head_width)

    def attend_block(block_index):
        row_start = block_index * block_rows
        query_block = lax.dynamic_slice_in_dim(queries_3d, row_start, block_rows, 0)
        label_block = lax.dynamic_slice_in_dim(query_labels, row_start, block_rows, 0)
        query_pos = row_start + jnp.arange(block_rows)
        scores = (
            jnp.einsum("qhd,khd->hqk", query_block, band_keys, preferred_element_type=jnp.float32)
            * score_scale
        )
        nearby = (
            (key_pos[None, :] <= query_pos[:, None])
            & (key_pos[None, :] > query_pos[:, None] - band_width)
            & key_valid[None, :]
        )
        same_span = (label_block[:, None] > 0) & (label_block[:, None] == key_labels[None, :])
        visible = nearby | same_span
        scores = jnp.where(visible[None], scores, -1e30)
        top_score = jnp.max(scores, axis=-1, keepdims=True)
        weights = jnp.exp(scores - top_score)
        totals = jnp.sum(weights, axis=-1)
        mixed_out = jnp.einsum(
            "hqk,khd->qhd",
            weights.astype(jnp.bfloat16),
            band_values,
            preferred_element_type=jnp.float32,
        )
        return mixed_out / jnp.transpose(totals)[:, :, None]

    blocks = lax.map(attend_block, jnp.arange(seg_rows // block_rows))
    return blocks.reshape(seg_rows, head_count, head_width)


def body(queries, keys, values, span_bounds, mem_decay, mem_gate, out_weight):
    seg_rows = queries.shape[0]
    head_count = mem_gate.shape[0]
    head_width = queries.shape[1] // head_count
    band_width = BAND
    shard_index = lax.axis_index("seq")
    prev_keys, prev_values = from_behind(
        (keys[seg_rows - band_width :], values[seg_rows - band_width :]), "seq", 1
    )
    key_feats = feature_map(keys.astype(jnp.float32)).reshape(seg_rows, head_count, head_width)
    value_rows = values.astype(jnp.float32).reshape(seg_rows, head_count, head_width)
    state = jnp.einsum("thd,the->hde", key_feats, value_rows, precision=HIGHEST_PRECISION)
    feat_sum = jnp.sum(key_feats, axis=0)
    cumulative = jnp.cumsum(jnp.log(mem_decay), axis=0)
    before = lax.dynamic_index_in_dim(
        cumulative, jnp.maximum(shard_index - 1, 0), 0, keepdims=False
    )
    part_state = lax.all_gather(state[None], "seq", axis=0, tiled=True)
    part_sum = lax.all_gather(feat_sum[None], "seq", axis=0, tiled=True)
    piece_count = part_state.shape[0]
    piece_index = jnp.arange(piece_count)
    factor = jnp.where(
        (piece_index < shard_index)[:, None],
        jnp.exp(jnp.minimum(before[None, :] - cumulative, 0.0)),
        0.0,
    )
    memory = jnp.einsum("nh,nhde->hde", factor, part_state, precision=HIGHEST_PRECISION)
    feat_total = jnp.einsum("nh,nhd->hd", factor, part_sum, precision=HIGHEST_PRECISION)
    query_feats = feature_map(queries.astype(jnp.float32)).reshape(seg_rows, head_count, head_width)
    numer = jnp.einsum("thd,hde->the", query_feats, memory, precision=HIGHEST_PRECISION)
    denom = jnp.einsum("thd,hd->th", query_feats, feat_total, precision=HIGHEST_PRECISION) + 1.0
    readout = numer / denom[:, :, None]
    own_spans = lax.dynamic_slice_in_dim(span_bounds, shard_index * SPAN_DEV, SPAN_DEV, 0)
    positions = shard_index * seg_rows + jnp.arange(seg_rows)
    inside = (positions[:, None] >= own_spans[None, :, 0]) & (
        positions[:, None] < own_spans[None, :, 1]
    )
    slot_ids = (jnp.arange(SPAN_DEV) + 1)[None, :]
    query_labels = jnp.sum(inside.astype(jnp.int32) * slot_ids, axis=1)
    key_labels = jnp.concatenate([jnp.zeros((band_width,), jnp.int32), query_labels])
    band_keys = jnp.concatenate([prev_keys, keys], axis=0).reshape(
        band_width + seg_rows, head_count, head_width
    )
    band_values = jnp.concatenate([prev_values, values], axis=0).reshape(
        band_width + seg_rows, head_count, head_width
    )
    queries_3d = queries.reshape(seg_rows, head_count, head_width)
    local = local_attention(
        queries_3d, band_keys, band_values, query_labels, key_labels, shard_index, band_width
    )
    gate = jax.nn.sigmoid(mem_gate)[None, :, None]
    attended = (
        (gate * readout + (1.0 - gate) * local)
        .astype(jnp.bfloat16)
        .reshape(seg_rows, head_count * head_width)
    )
    gathered = lax.all_gather(attended, "head", axis=1, tiled=True)
    columns = lax.all_to_all(out_weight, "head", split_axis=1, concat_axis=0, tiled=True)
    mixed = jnp.dot(gathered, columns, preferred_element_type=jnp.float32)
    return mixed.astype(jnp.bfloat16)


def solution(mesh):
    return jax.shard_map(
        body,
        mesh=mesh,
        in_specs=(
            P("seq", "head"),
            P("seq", "head"),
            P("seq", "head"),
            P(),
            P(None, "head"),
            P("head"),
            P("head", None),
        ),
        out_specs=P("seq", "head"),
        check_vma=False,
    )
```

profile of v0, /device:TPU:0, one launch (start us, length us, event | category | flops | bytes accessed | tf_op | source)
XLA Modules:
  0.0 270.6 jit_solution(7278276117064473592)
XLA Ops:
  6.5 1.6 copy.56
  9.0 5.7 %collective-permute-start = (bf16[512,512]{0,1:T(8,128)(2,1)}, bf16[512,512]{0,1:T(8,128)(2,1)}, u32[]{:S(2)}, u32[]{:S(2)}) collective-permute-start(bf16[512,512]{0,1:T(8,128)(2,1)} %slice.16), channel_id=1, source_target_pairs={{0,4},{4,8},{8,12},{12,16},{16,20},{20,24},{24,28},{1,5},{5,9},{9,... | collective-permute-start | bytes 1572872 | tf_op jit(solution)/shard_map/ppermute | solution.py:15
  16.1 3.5 %collective-permute-start.1 = (bf16[512,512]{0,1:T(8,128)(2,1)}, bf16[512,512]{0,1:T(8,128)(2,1)}, u32[]{:S(2)}, u32[]{:S(2)}) collective-permute-start(bf16[512,512]{0,1:T(8,128)(2,1)} %slice.17), channel_id=1, source_target_pairs={{0,4},{4,8},{8,12},{12,16},{16,20},{20,24},{24,28},{1,5},{5,9},{9,... | collective-permute-start | bytes 1572872 | tf_op jit(solution)/shard_map/ppermute | solution.py:15
  19.6 1.8 fusion.35
  21.4 1.8 copy.75
  23.2 3.8 %fusion.29 = f32[4,128,128]{2,1,0:T(8,128)} fusion(f32[1024,4,128]{0,2,1:T(8,128)} %bitcast.87, bf16[1024,512]{1,0:T(8,128)(2,1)} %param.11), kind=kOutput, calls=%fused_computation.42 | convolution fusion | flops 805306368 | bytes 3407872 | tf_op jit(solution)/shard_map/thd,the->hde/dot_general | solution.py:75
  27.1 37.5 %all_gather.10 = f32[8,4,128]{2,1,0:T(4,128)S(1)} all-gather(f32[1,4,128]{2,1,0:T(4,128)S(1)} %bitcast.97), channel_id=1, replica_groups=mesh['seq'=8,'head'=4] {'seq'}, dimensions={0}, use_global_device_ids=true | all-gather | bytes 18432 | tf_op jit(solution)/shard_map/all_gather | solution.py:82
  64.7 1.8 fusion.22
  66.5 1.9 copy.81
  70.3 2.3 copy.55
  72.6 2.6 pad_maximum_fusion
  75.2 1.9 copy.61
  77.2 2.3 pad_maximum_fusion.1
  79.5 2.6 copy.62
  82.1 77.2 %while.14 = (s32[]{:T(128)}, f32[2,512,4,128]{1,0,3,2:T(2,128)}, s32[2]{0:T(128)S(1)}, s32[1024]{0:T(1024)S(1)}, s32[1536]{0:T(1024)S(1)}, /*index=5*/bf16[1024,...) while((s32[]{:T(128)}, f32[2,512,4,128]{1,0,3,2:T(2,128)}, ...), condition=%wide.region_6.7_spmd.clone.clone, body=%wide.region_3.6_spmd.clone.clone.sunk | while | flops 1650986496 | bytes 49885384 | solution.py:60
  84.9 4.1 %fusion.57 = (f32[4,512]{1,0:T(4,128)S(1)}, f32[4,512,1536]{2,1,0:T(8,128)S(1)}) fusion(pred[512,1536]{1,0:T(8,128)(4,1)S(1)} %and_or_fusion.2, bf16[1536,4,128]{2,0,1:T(8,128)(2,1)S(1)} %get-tuple-element.345, bf16[1024,4,128]{0,2,1:T(8,128)(2,1)} %get-tuple-element.344, s32[]{:T(128)S(6)} %select_n.64), kind=kOutput, calls=%fused_computation.4.clone.1 | convolution fusion | flops 814741504 | bytes 15474692 | tf_op jit(solution)/shard_map/while/body/eval_jaxpr/qhd,khd->hqk/dot_general | solution.py:38
  89.0 3.6 %fusion.58 = f32[4,512]{1,0:T(4,128)S(1)} fusion(f32[4,512,1536]{2,1,0:T(8,128)S(1)} %get-tuple-element.311, f32[4,512]{1,0:T(4,128)S(1)} %get-tuple-element.312, pred[512,1536]{1,0:T(8,128)(4,1)S(1)} %and_or_fusion.2), kind=kLoop, calls=%fused_computation.5.clone.1 | loop fusion | flops 12580864 | bytes 13385728 | tf_op jit(solution)/shard_map/while/body/eval_jaxpr/reduce_sum | solution.py:51
  92.7 6.0 %divide_bitcast_fusion.2 = f32[1,512,4,128]{3,1,2,0:T(8,128)} fusion(bf16[1536,4,128]{2,0,1:T(8,128)(2,1)} %get-tuple-element.346, f32[4,512,1536]{2,1,0:T(8,128)S(1)} %get-tuple-element.311, f32[4,512]{1,0:T(4,128)S(1)} %get-tuple-element.312, pred[512,1536]{1,0:T(8,128)(4,1)S(1)} %and_or_fusion.2, f32[512,4]{0,1:T(4,128)S(1)} %bitcast.94), kind=kOutput, calls=%fused_computation.11.clone.1 | convolution fusion | flops 818151424 | bytes 16007168 | tf_op jit(solution)/shard_map/while/body/eval_jaxpr/hqk,khd->qhd/dot_general | solution.py:52
  98.7 2.4 copy.93
  101.1 19.6 %dynamic_update_slice.10 = f32[2,512,4,128]{1,0,3,2:T(2,128)} dynamic-update-slice(f32[2,512,4,128]{1,0,3,2:T(2,128)} %get-tuple-element.327, f32[1,512,4,128]{1,0,3,2:T(1,128)S(1)} %copy.93, s32[]{:T(128)} %get-tuple-element.326, s32[]{:T(128)} %constant.90.clone.1..sunk, s32[]{:T(128)} %constant.90.clone.1..sunk, s32[]{:T(128)} %constant.90.clone.1..sunk) | dynamic-update-slice | bytes 2097156 | tf_op jit(solution)/shard_map/while/body/jit(dynamic_update_index_in_dim)/dynamic_update_slice | solution.py:60
  123.5 4.1 %fusion.57 = (f32[4,512]{1,0:T(4,128)S(1)}, f32[4,512,1536]{2,1,0:T(8,128)S(1)}) fusion(pred[512,1536]{1,0:T(8,128)(4,1)S(1)} %and_or_fusion.2, bf16[1536,4,128]{2,0,1:T(8,128)(2,1)S(1)} %get-tuple-element.345, bf16[1024,4,128]{0,2,1:T(8,128)(2,1)} %get-tuple-element.344, s32[]{:T(128)S(6)} %select_n.64), kind=kOutput, calls=%fused_computation.4.clone.1 | convolution fusion | flops 814741504 | bytes 15474692 | tf_op jit(solution)/shard_map/while/body/eval_jaxpr/qhd,khd->hqk/dot_general | solution.py:38
  127.6 3.6 %fusion.58 = f32[4,512]{1,0:T(4,128)S(1)} fusion(f32[4,512,1536]{2,1,0:T(8,128)S(1)} %get-tuple-element.311, f32[4,512]{1,0:T(4,128)S(1)} %get-tuple-element.312, pred[512,1536]{1,0:T(8,128)(4,1)S(1)} %and_or_fusion.2), kind=kLoop, calls=%fused_computation.5.clone.1 | loop fusion | flops 12580864 | bytes 13385728 | tf_op jit(solution)/shard_map/while/body/eval_jaxpr/reduce_sum | solution.py:51
  131.3 6.0 %divide_bitcast_fusion.2 = f32[1,512,4,128]{3,1,2,0:T(8,128)} fusion(bf16[1536,4,128]{2,0,1:T(8,128)(2,1)} %get-tuple-element.346, f32[4,512,1536]{2,1,0:T(8,128)S(1)} %get-tuple-element.311, f32[4,512]{1,0:T(4,128)S(1)} %get-tuple-element.312, pred[512,1536]{1,0:T(8,128)(4,1)S(1)} %and_or_fusion.2, f32[512,4]{0,1:T(4,128)S(1)} %bitcast.94), kind=kOutput, calls=%fused_computation.11.clone.1 | convolution fusion | flops 818151424 | bytes 16007168 | tf_op jit(solution)/shard_map/while/body/eval_jaxpr/hqk,khd->qhd/dot_general | solution.py:52
  137.3 2.4 copy.93
  139.7 19.6 %dynamic_update_slice.10 = f32[2,512,4,128]{1,0,3,2:T(2,128)} dynamic-update-slice(f32[2,512,4,128]{1,0,3,2:T(2,128)} %get-tuple-element.327, f32[1,512,4,128]{1,0,3,2:T(1,128)S(1)} %copy.93, s32[]{:T(128)} %get-tuple-element.326, s32[]{:T(128)} %constant.90.clone.1..sunk, s32[]{:T(128)} %constant.90.clone.1..sunk, s32[]{:T(128)} %constant.90.clone.1..sunk) | dynamic-update-slice | bytes 2097156 | tf_op jit(solution)/shard_map/while/body/jit(dynamic_update_index_in_dim)/dynamic_update_slice | solution.py:60
  159.3 4.0 %reshape.179 = f32[1024,4,128]{0,2,1:T(8,128)} reshape(f32[2,512,4,128]{1,0,3,2:T(2,128)} %get-tuple-element.133) | data formatting | bytes 4194304 | tf_op jit(solution)/shard_map/reshape | solution.py:61
  163.3 4.6 %fusion.27 = f32[4,1,128,128]{3,1,2,0:T(1,128)S(1)} fusion(f32[8,4,1,1]{0,2,3,1:T(1,128)S(1)} %bitcast.96, f32[8,4,128,128]{3,2,1,0:T(8,128)} %bitcast.91), kind=kOutput, calls=%fused_computation.36 | convolution fusion | flops 6291456 | bytes 2359424 | tf_op jit(solution)/shard_map/nh,nhde->hde/dot_general | solution.py:90
  167.9 4.8 %fusion.26 = bf16[1024,4,128]{0,2,1:T(8,128)(2,1)} fusion(f32[1024,4,128]{0,2,1:T(8,128)} %reshape.179, f32[4,128,128]{2,1,0:T(8,128)S(1)} %bitcast.93, f32[1024,4,128]{0,2,1:T(8,128)S(1)} %bitcast.86, f32[4]{0:T(128)S(1)} %get-tuple-element.236, f32[1024,4]{0,1:T(4,128)S(1)} %fusion.32, f32[4]{0:T(128)S(1)} %get-tuple-element.237), kind=kOutput, calls=%fused_computation.35 | convolution fusion | flops 807927808 | bytes 5521440 | tf_op jit(solution)/shard_map/thd,hde->the/dot_general | solution.py:93
  172.7 6.6 %copy.64 = bf16[512,4096]{0,1:T(8,128)(2,1)} copy(bf16[512,4096]{1,0:T(8,128)(2,1)} %param.15) | data formatting | bytes 8388608 | tf_op args[6]
  179.3 68.7 %all_to_all.19 = bf16[512,4,1024]{0,2,1:T(8,128)(2,1)} all-to-all(bf16[512,4,1024]{0,2,1:T(8,128)(2,1)} %bitcast.84), channel_id=1, replica_groups=mesh['seq'=8,'head'=4] {'head'}, dimensions={1} | all-to-all | bytes 8388608 | tf_op jit(solution)/shard_map/all_to_all | solution.py:121
  248.0 6.3 %copy.65 = bf16[4,512,1024]{2,1,0:T(8,128)(2,1)} copy(bf16[4,512,1024]{1,2,0:T(8,128)(2,1)} %bitcast.83) | data formatting | bytes 8388608 | tf_op jit(solution)/shard_map/all_to_all | solution.py:121
  254.3 9.4 %convolution_convert_fusion = bf16[1024,1024]{1,0:T(8,128)(2,1)} fusion(bf16[1024,2048]{0,1:T(8,128)(2,1)} %all-gather.4.cloned.1.call-done, bf16[2048,1024]{1,0:T(8,128)(2,1)} %bitcast.90), kind=kOutput, calls=%fused_computation.38 | convolution fusion | flops 4296015872 | bytes 10485760 | tf_op jit(solution)/shard_map/dot_general | solution.py:122
  (58 shorter events, 8.6 us)
Async XLA Ops:
  6.5 20.5 %copy-start = (s32[16,2]{0,1:T(2,128)S(1)}, s32[16,2]{0,1:T(2,128)}, u32[]{:S(2)}) copy-start(s32[16,2]{0,1:T(2,128)} %param.12) | copy-start | bytes 388
  6.5 8.2 %copy-start.6 = (bf16[1024,512]{1,0:T(8,128)(2,1)S(1)}, bf16[1024,512]{1,0:T(8,128)(2,1)}, u32[]{:S(2)}) copy-start(bf16[1024,512]{1,0:T(8,128)(2,1)} %param.11) | copy-start | bytes 3145732
  6.5 156.8 %all-gather.6.cloned.1.call-start = ((), (), s32[]{:S(2)}) async-start(), calls=%async_computation.2 | async-start | bytes 2359296 | tf_op jit(solution)/shard_map/all_gather | solution.py:81
  8.1 8.0 %copy-start.4 = (bf16[1024,512]{0,1:T(8,128)(2,1)}, bf16[1024,512]{0,1:T(8,128)(2,1)S(1)}, u32[]{:S(2)}) copy-start(bf16[1024,512]{0,1:T(8,128)(2,1)S(1)} %copy.56) | copy-start | bytes 3145732
  9.0 63.6 %collective-permute-start = (bf16[512,512]{0,1:T(8,128)(2,1)}, bf16[512,512]{0,1:T(8,128)(2,1)}, u32[]{:S(2)}, u32[]{:S(2)}) collective-permute-start(bf16[512,512]{0,1:T(8,128)(2,1)} %slice.16), channel_id=1, source_target_pairs={{0,4},{4,8},{8,12},{12,16},{16,20},{20,24},{24,28},{1,5},{5,9},{9,... | collective-permute-start | bytes 1572872 | tf_op jit(solution)/shard_map/ppermute | solution.py:15
  16.1 61.0 %collective-permute-start.1 = (bf16[512,512]{0,1:T(8,128)(2,1)}, bf16[512,512]{0,1:T(8,128)(2,1)}, u32[]{:S(2)}, u32[]{:S(2)}) collective-permute-start(bf16[512,512]{0,1:T(8,128)(2,1)} %slice.17), channel_id=1, source_target_pairs={{0,4},{4,8},{8,12},{12,16},{16,20},{20,24},{24,28},{1,5},{5,9},{9,... | collective-permute-start | bytes 1572872 | tf_op jit(solution)/shard_map/ppermute | solution.py:15
  23.2 4.0 %copy-start.7 = (f32[8,4]{0,1:T(4,128)S(1)}, f32[8,4]{0,1:T(4,128)}, u32[]{:S(2)}) copy-start(f32[8,4]{0,1:T(4,128)} %param.13) | copy-start | bytes 388
  23.2 41.5 %copy-start.5 = (bf16[1024,512]{1,0:T(8,128)(2,1)S(1)}, bf16[1024,512]{1,0:T(8,128)(2,1)}, u32[]{:S(2)}) copy-start(bf16[1024,512]{1,0:T(8,128)(2,1)} %param.9) | copy-start | bytes 3145732
  27.0 227.4 %all-gather.4.cloned.1.call-start = ((), (), s32[]{:S(2)}) async-start(), calls=%async_computation.1 | async-start | bytes 5242880 | tf_op jit(solution)/shard_map/all_gather | solution.py:120
  68.4 4.2 %copy-start.2 = (f32[1024,512]{0,1:T(8,128)}, f32[1024,512]{0,1:T(8,128)S(1)}, u32[]{:S(2)}) copy-start(f32[1024,512]{0,1:T(8,128)S(1)} %copy.81) | copy-start | bytes 6291460
  68.4 1.7 copy-start.8
  163.3 4.6 %copy-start.3 = (f32[1024,512]{0,1:T(8,128)S(1)}, f32[1024,512]{0,1:T(8,128)}, u32[]{:S(2)}) copy-start(f32[1024,512]{0,1:T(8,128)} %copy-done.2) | copy-start | bytes 6291460
  254.3 9.4 %copy-start.1 = (s32[16,2]{0,1:T(2,128)S(1)}, s32[16,2]{0,1:T(2,128)}, u32[]{:S(2)}) copy-start(s32[16,2]{0,1:T(2,128)} %param.12) | copy-start | bytes 388
Sparse Core Ops, SparseCore 0:
  27.1 49.7 all-gather.5
  172.8 46.6 all-gather.3
where the time goes:
time: 274 us; the launch traced here: 271 us
  blocking collectives  106 us (39%)
  local copies, waits for them, and re-layouts  76.8 us (28%)
  matrix products  44 us (16%)
  other arithmetic  19.3 us (7%)
  between operations  13.6 us (5%)
  starting transfers between devices  9.21 us (3%)
    all_to_all x1, blocking collectives, body(): lax.all_to_all(out_weight, 'head', split_axis=1, concat_axis=0, tiled=True)  68.7 us
    dynamic_update_slice x4, local copies, waits for them, and re-layouts, local_attention(): blocks = lax.map(attend_block, jnp.arange(seg_rows // block_rows))  44 us
    all_gather x1, blocking collectives, body(): part_sum = lax.all_gather(feat_sum[None], 'seq', axis=0, tiled=True)  37.5 us
    unnamed x24, local copies, waits for them, and re-layouts  15.5 us
    dot_general x2, matrix products, attend_block(): jnp.einsum('hqk,khd->qhd', weights.astype(jnp.bfloat16), band_values, pre...  12 us
    dot_general x1, matrix products, body(): mixed = jnp.dot(gathered, columns, preferred_element_type=jnp.float32)  9.37 us
    ppermute x2, starting transfers between devices, from_behind(): return lax.ppermute(block, axis, route)  9.17 us
    dot_general x2, matrix products, attend_block(): jnp.einsum('qhd,khd->hqk', query_block, band_keys, preferred_element_type...  8.27 us
  transfers between devices with their start and end apart: 4, of which 0 were waited for; matrix products, arithmetic and copies ran while one was open for 44% of the time, Pallas kernels for 0%

commit v1 on v0

--- a/solution.py
+++ b/solution.py
@@ -79,7 +79,6 @@
         cumulative, jnp.maximum(shard_index - 1, 0), 0, keepdims=False
     )
     part_state = lax.all_gather(state[None], "seq", axis=0, tiled=True)
-    part_sum = lax.all_gather(feat_sum[None], "seq", axis=0, tiled=True)
     piece_count = part_state.shape[0]
     piece_index = jnp.arange(piece_count)
     factor = jnp.where(
@@ -88,7 +87,33 @@
         0.0,
     )
     memory = jnp.einsum("nh,nhde->hde", factor, part_state, precision=HIGHEST_PRECISION)
-    feat_total = jnp.einsum("nh,nhd->hd", factor, part_sum, precision=HIGHEST_PRECISION)
+
+    def create_racks(arr, inputs):
+        item_now, z_new, clean = (lax.axis_size("seq"), lax.axis_index("seq"), arr.shape[0])
+        leaves = []
+        for at in range(item_now):
+            leaves.append((at, (at + 1) % item_now))
+        parts_out, response = (arr, None)
+        for dev_i in range(item_now):
+            arr_now = (
+                lax.ppermute(parts_out, perm=leaves, axis_name="seq")
+                if dev_i < item_now - 1
+                else None
+            )
+            plain = inputs(parts_out, (z_new - dev_i) % item_now * clean)
+            response = plain if response is None else response + plain
+            parts_out = arr_now
+        return response
+
+    feat_total = create_racks(
+        feat_sum[None],
+        lambda part, offset: jnp.einsum(
+            "nh,nhd->hd",
+            lax.dynamic_slice_in_dim(factor, offset, part.shape[0], axis=0),
+            part,
+            precision=HIGHEST_PRECISION,
+        ),
+    )
     query_feats = feature_map(queries.astype(jnp.float32)).reshape(seg_rows, head_count, head_width)
     numer = jnp.einsum("thd,hde->the", query_feats, memory, precision=HIGHEST_PRECISION)
     denom = jnp.einsum("thd,hd->th", query_feats, feat_total, precision=HIGHEST_PRECISION) + 1.0

time: 274 us -> 282 us (1.029)
  waiting for transfers between devices: 0.04 us -> 41.3 us
  blocking collectives: 106 us -> 68.8 us
  starting transfers between devices: 9.21 us -> 12.4 us
    ppermute x0 -> x7, waiting for transfers between devices: none -> 41.3 us  [create_racks(): lax.ppermute(parts_out, perm=leaves, axis_name='seq')]
    all_gather x1 -> x0, blocking collectives: 37.5 us -> none  [body(): part_sum = lax.all_gather(feat_sum[None], 'seq', axis=0, tiled=True)]
    ppermute x0 -> x7, starting transfers between devices: none -> 3.2 us  [create_racks(): lax.ppermute(parts_out, perm=leaves, axis_name='seq')]
    unnamed x24 -> x22, local copies, waits for them, and re-layouts: 15.5 us -> 15.5 us
  transfers between devices with their start and end apart: 4 -> 11, of which waited for: 0 -> 7; matrix products, arithmetic and copies ran while one was open for 44% -> 43% of each run, Pallas kernels for 0% -> 0%
where the time goes in v1:
time: 282 us; the launch traced here: 279 us
  local copies, waits for them, and re-layouts  77 us (27%)
  blocking collectives  68.8 us (24%)
  matrix products  45.5 us (16%)
  waiting for transfers between devices  41.3 us (15%)
  other arithmetic  18.9 us (7%)
  between operations  13.5 us (5%)
  starting transfers between devices  12.4 us (4%)
    all_to_all x1, blocking collectives, body(): lax.all_to_all(out_weight, 'head', split_axis=1, concat_axis=0, tiled=True)  68.8 us
    dynamic_update_slice x4, local copies, waits for them, and re-layouts, local_attention(): blocks = lax.map(attend_block, jnp.arange(seg_rows // block_rows))  44 us
    ppermute x7, waiting for transfers between devices, create_racks(): lax.ppermute(parts_out, perm=leaves, axis_name='seq')  41.3 us
    unnamed x22, local copies, waits for them, and re-layouts  15.5 us
    dot_general x2, matrix products, attend_block(): jnp.einsum('hqk,khd->qhd', weights.astype(jnp.bfloat16), band_values, pre...  12.1 us
    dot_general x1, matrix products, body(): mixed = jnp.dot(gathered, columns, preferred_element_type=jnp.float32)  9.37 us
    ppermute x2, starting transfers between devices, from_behind(): return lax.ppermute(block, axis, route)  9.18 us
    dot_general x2, matrix products, attend_block(): jnp.einsum('qhd,khd->hqk', query_block, band_keys, preferred_element_type...  8.27 us
  transfers between devices with their start and end apart: 11, of which 7 were waited for; matrix products, arithmetic and copies ran while one was open for 43% of the time, Pallas kernels for 0%

profile of v1, /device:TPU:0, one launch (start us, length us, event | category | flops | bytes accessed | tf_op | source)
XLA Modules:
  0.0 278.6 jit_solution(2424444318245024506)
XLA Ops:
  9.0 5.7 %collective-permute-start.7 = (bf16[512,512]{0,1:T(8,128)(2,1)}, bf16[512,512]{0,1:T(8,128)(2,1)}, u32[]{:S(2)}, u32[]{:S(2)}) collective-permute-start(bf16[512,512]{0,1:T(8,128)(2,1)} %slice.16), channel_id=1, source_target_pairs={{0,4},{4,8},{8,12},{12,16},{16,20},{20,24},{24,28},{1,5},{5,9},{9,... | collective-permute-start | bytes 1572872 | tf_op jit(solution)/shard_map/ppermute | solution.py:15
  16.1 3.5 %collective-permute-start.8 = (bf16[512,512]{0,1:T(8,128)(2,1)}, bf16[512,512]{0,1:T(8,128)(2,1)}, u32[]{:S(2)}, u32[]{:S(2)}) collective-permute-start(bf16[512,512]{0,1:T(8,128)(2,1)} %slice.17), channel_id=1, source_target_pairs={{0,4},{4,8},{8,12},{12,16},{16,20},{20,24},{24,28},{1,5},{5,9},{9,... | collective-permute-start | bytes 1572872 | tf_op jit(solution)/shard_map/ppermute | solution.py:15
  23.2 3.7 %fusion.29 = f32[4,128,128]{2,1,0:T(8,128)} fusion(f32[1024,4,128]{0,2,1:T(8,128)} %bitcast.124, bf16[1024,512]{1,0:T(8,128)(2,1)} %param.11), kind=kOutput, calls=%fused_computation.41 | convolution fusion | flops 805306368 | bytes 3407872 | tf_op jit(solution)/shard_map/thd,the->hde/dot_general | solution.py:75
  30.0 9.3 %collective-permute-done = f32[1,4,128]{2,1,0:T(4,128)S(1)} collective-permute-done((f32[1,4,128]{2,1,0:T(4,128)S(1)}, f32[1,4,128]{2,1,0:T(4,128)S(1)}, u32[]{:S(2)}, u32[]{:S(2)}) %collective-permute-start) | collective-permute-done | bytes 2080 | tf_op jit(solution)/shard_map/ppermute | solution.py:99
  39.2 2.5 collective-permute-start.1
  41.7 4.6 %collective-permute-done.1 = f32[1,4,128]{2,1,0:T(4,128)S(1)} collective-permute-done((f32[1,4,128]{2,1,0:T(4,128)S(1)}, f32[1,4,128]{2,1,0:T(4,128)S(1)}, u32[]{:S(2)}, u32[]{:S(2)}) %collective-permute-start.1) | collective-permute-done | bytes 2080 | tf_op jit(solution)/shard_map/ppermute | solution.py:99
  46.4 6.3 %collective-permute-done.2 = f32[1,4,128]{2,1,0:T(4,128)S(1)} collective-permute-done((f32[1,4,128]{2,1,0:T(4,128)S(1)}, f32[1,4,128]{2,1,0:T(4,128)S(1)}, u32[]{:S(2)}, u32[]{:S(2)}) %collective-permute-start.2) | collective-permute-done | bytes 2080 | tf_op jit(solution)/shard_map/ppermute | solution.py:99
  55.0 4.0 %collective-permute-done.3 = f32[1,4,128]{2,1,0:T(4,128)S(1)} collective-permute-done((f32[1,4,128]{2,1,0:T(4,128)S(1)}, f32[1,4,128]{2,1,0:T(4,128)S(1)}, u32[]{:S(2)}, u32[]{:S(2)}) %collective-permute-start.3) | collective-permute-done | bytes 2080 | tf_op jit(solution)/shard_map/ppermute | solution.py:99
  59.0 6.5 %collective-permute-done.4 = f32[1,4,128]{2,1,0:T(4,128)S(1)} collective-permute-done((f32[1,4,128]{2,1,0:T(4,128)S(1)}, f32[1,4,128]{2,1,0:T(4,128)S(1)}, u32[]{:S(2)}, u32[]{:S(2)}) %collective-permute-start.4) | collective-permute-done | bytes 2080 | tf_op jit(solution)/shard_map/ppermute | solution.py:99
  65.5 6.5 %collective-permute-done.5 = f32[1,4,128]{2,1,0:T(4,128)S(1)} collective-permute-done((f32[1,4,128]{2,1,0:T(4,128)S(1)}, f32[1,4,128]{2,1,0:T(4,128)S(1)}, u32[]{:S(2)}, u32[]{:S(2)}) %collective-permute-start.5) | collective-permute-done | bytes 2080 | tf_op jit(solution)/shard_map/ppermute | solution.py:99
  74.1 4.2 %collective-permute-done.6 = f32[1,4,128]{2,1,0:T(4,128)S(1)} collective-permute-done((f32[1,4,128]{2,1,0:T(4,128)S(1)}, f32[1,4,128]{2,1,0:T(4,128)S(1)}, u32[]{:S(2)}, u32[]{:S(2)}) %collective-permute-start.6) | collective-permute-done | bytes 2080 | tf_op jit(solution)/shard_map/ppermute | solution.py:99
  78.3 2.7 fusion.51
  85.3 2.3 pad_maximum_fusion.1
  87.6 2.6 copy.62
  90.2 77.0 %while.14 = (s32[]{:T(128)}, f32[2,512,4,128]{1,0,3,2:T(2,128)}, s32[2]{0:T(128)S(1)}, s32[1024]{0:T(1024)S(1)}, s32[1536]{0:T(1024)S(1)}, /*index=5*/bf16[1024,...) while((s32[]{:T(128)}, f32[2,512,4,128]{1,0,3,2:T(2,128)}, ...), condition=%wide.region_6.7_spmd.clone.clone, body=%wide.region_3.6_spmd.clone.clone.sunk | while | flops 1650986496 | bytes 49885392 | solution.py:60
  92.9 4.1 %fusion.71 = (f32[4,512]{1,0:T(4,128)S(1)}, f32[4,512,1536]{2,1,0:T(8,128)S(1)}) fusion(pred[512,1536]{1,0:T(8,128)(4,1)S(1)} %and_or_fusion.2, bf16[1536,4,128]{2,0,1:T(8,128)(2,1)S(1)} %get-tuple-element.353, bf16[1024,4,128]{0,2,1:T(8,128)(2,1)} %get-tuple-element.352, s32[]{:T(128)S(6)} %select_n.139), kind=kOutput, calls=%fused_computation.4.clone.1 | convolution fusion | flops 814741504 | bytes 15474692 | tf_op jit(solution)/shard_map/while/body/eval_jaxpr/qhd,khd->hqk/dot_general | solution.py:38
  97.0 3.6 %fusion.72 = f32[4,512]{1,0:T(4,128)S(1)} fusion(f32[4,512,1536]{2,1,0:T(8,128)S(1)} %get-tuple-element.319, f32[4,512]{1,0:T(4,128)S(1)} %get-tuple-element.320, pred[512,1536]{1,0:T(8,128)(4,1)S(1)} %and_or_fusion.2), kind=kLoop, calls=%fused_computation.5.clone.1 | loop fusion | flops 12580864 | bytes 13385728 | tf_op jit(solution)/shard_map/while/body/eval_jaxpr/reduce_sum | solution.py:51
  100.7 6.0 %divide_bitcast_fusion.2 = f32[1,512,4,128]{3,1,2,0:T(8,128)} fusion(bf16[1536,4,128]{2,0,1:T(8,128)(2,1)} %get-tuple-element.354, f32[4,512,1536]{2,1,0:T(8,128)S(1)} %get-tuple-element.319, f32[4,512]{1,0:T(4,128)S(1)} %get-tuple-element.320, pred[512,1536]{1,0:T(8,128)(4,1)S(1)} %and_or_fusion.2, f32[512,4]{0,1:T(4,128)S(1)} %bitcast.131), kind=kOutput, calls=%fused_computation.11.clone.1 | convolution fusion | flops 818151424 | bytes 16007168 | tf_op jit(solution)/shard_map/while/body/eval_jaxpr/hqk,khd->qhd/dot_general | solution.py:52
  106.7 2.4 copy.88
  109.1 19.6 %dynamic_update_slice.10 = f32[2,512,4,128]{1,0,3,2:T(2,128)} dynamic-update-slice(f32[2,512,4,128]{1,0,3,2:T(2,128)} %get-tuple-element.335, f32[1,512,4,128]{1,0,3,2:T(1,128)S(1)} %copy.88, s32[]{:T(128)S(6)} %copy.92, s32[]{:T(128)} %constant.139.clone.1..sunk, s32[]{:T(128)} %constant.139.clone.1..sunk, s32[]{:T(128)} %constant.139.clone.1..sunk) | dynamic-update-slice | bytes 2097156 | tf_op jit(solution)/shard_map/while/body/jit(dynamic_update_index_in_dim)/dynamic_update_slice | solution.py:60
  131.4 4.1 %fusion.71 = (f32[4,512]{1,0:T(4,128)S(1)}, f32[4,512,1536]{2,1,0:T(8,128)S(1)}) fusion(pred[512,1536]{1,0:T(8,128)(4,1)S(1)} %and_or_fusion.2, bf16[1536,4,128]{2,0,1:T(8,128)(2,1)S(1)} %get-tuple-element.353, bf16[1024,4,128]{0,2,1:T(8,128)(2,1)} %get-tuple-element.352, s32[]{:T(128)S(6)} %select_n.139), kind=kOutput, calls=%fused_computation.4.clone.1 | convolution fusion | flops 814741504 | bytes 15474692 | tf_op jit(solution)/shard_map/while/body/eval_jaxpr/qhd,khd->hqk/dot_general | solution.py:38
  135.5 3.6 %fusion.72 = f32[4,512]{1,0:T(4,128)S(1)} fusion(f32[4,512,1536]{2,1,0:T(8,128)S(1)} %get-tuple-element.319, f32[4,512]{1,0:T(4,128)S(1)} %get-tuple-element.320, pred[512,1536]{1,0:T(8,128)(4,1)S(1)} %and_or_fusion.2), kind=kLoop, calls=%fused_computation.5.clone.1 | loop fusion | flops 12580864 | bytes 13385728 | tf_op jit(solution)/shard_map/while/body/eval_jaxpr/reduce_sum | solution.py:51
  139.2 6.0 %divide_bitcast_fusion.2 = f32[1,512,4,128]{3,1,2,0:T(8,128)} fusion(bf16[1536,4,128]{2,0,1:T(8,128)(2,1)} %get-tuple-element.354, f32[4,512,1536]{2,1,0:T(8,128)S(1)} %get-tuple-element.319, f32[4,512]{1,0:T(4,128)S(1)} %get-tuple-element.320, pred[512,1536]{1,0:T(8,128)(4,1)S(1)} %and_or_fusion.2, f32[512,4]{0,1:T(4,128)S(1)} %bitcast.131), kind=kOutput, calls=%fused_computation.11.clone.1 | convolution fusion | flops 818151424 | bytes 16007168 | tf_op jit(solution)/shard_map/while/body/eval_jaxpr/hqk,khd->qhd/dot_general | solution.py:52
  145.2 2.4 copy.88
  147.6 19.6 %dynamic_update_slice.10 = f32[2,512,4,128]{1,0,3,2:T(2,128)} dynamic-update-slice(f32[2,512,4,128]{1,0,3,2:T(2,128)} %get-tuple-element.335, f32[1,512,4,128]{1,0,3,2:T(1,128)S(1)} %copy.88, s32[]{:T(128)S(6)} %copy.92, s32[]{:T(128)} %constant.139.clone.1..sunk, s32[]{:T(128)} %constant.139.clone.1..sunk, s32[]{:T(128)} %constant.139.clone.1..sunk) | dynamic-update-slice | bytes 2097156 | tf_op jit(solution)/shard_map/while/body/jit(dynamic_update_index_in_dim)/dynamic_update_slice | solution.py:60
  167.2 4.1 %reshape.244 = f32[1024,4,128]{0,2,1:T(8,128)} reshape(f32[2,512,4,128]{1,0,3,2:T(2,128)} %get-tuple-element.133) | data formatting | bytes 4194304 | tf_op jit(solution)/shard_map/reshape | solution.py:61
  171.3 4.6 %fusion.27 = f32[4,1,128,128]{3,1,2,0:T(1,128)S(1)} fusion(f32[8,4,1,1]{0,2,3,1:T(1,128)S(1)} %bitcast.132, f32[8,4,128,128]{3,2,1,0:T(8,128)} %bitcast.128), kind=kOutput, calls=%fused_computation.36 | convolution fusion | flops 6291456 | bytes 2359424 | tf_op jit(solution)/shard_map/nh,nhde->hde/dot_general | solution.py:89
  175.9 4.8 %fusion.26 = bf16[1024,4,128]{0,2,1:T(8,128)(2,1)} fusion(f32[1024,4,128]{0,2,1:T(8,128)} %reshape.244, f32[4,128,128]{2,1,0:T(8,128)S(1)} %bitcast.130, f32[1024,4,128]{0,2,1:T(8,128)S(1)} %bitcast.123, f32[4]{0:T(128)S(1)} %get-tuple-element.244, f32[1024,4]{0,1:T(4,128)S(1)} %fusion.32, f32[4]{0:T(128)S(1)} %get-tuple-element.245), kind=kOutput, calls=%fused_computation.35 | convolution fusion | flops 807927808 | bytes 5521440 | tf_op jit(solution)/shard_map/thd,hde->the/dot_general | solution.py:118
  180.7 6.6 %copy.64 = bf16[512,4096]{0,1:T(8,128)(2,1)} copy(bf16[512,4096]{1,0:T(8,128)(2,1)} %param.15) | data formatting | bytes 8388608 | tf_op args[6]
  187.3 68.8 %all_to_all.19 = bf16[512,4,1024]{0,2,1:T(8,128)(2,1)} all-to-all(bf16[512,4,1024]{0,2,1:T(8,128)(2,1)} %bitcast.121), channel_id=1, replica_groups=mesh['seq'=8,'head'=4] {'head'}, dimensions={1} | all-to-all | bytes 8388608 | tf_op jit(solution)/shard_map/all_to_all | solution.py:146
  256.0 6.4 %copy.65 = bf16[4,512,1024]{2,1,0:T(8,128)(2,1)} copy(bf16[4,512,1024]{1,2,0:T(8,128)(2,1)} %bitcast.120) | data formatting | bytes 8388608 | tf_op jit(solution)/shard_map/all_to_all | solution.py:146
  262.4 9.4 %convolution_convert_fusion = bf16[1024,1024]{1,0:T(8,128)(2,1)} fusion(bf16[1024,2048]{0,1:T(8,128)(2,1)} %all-gather.4.cloned.1.call-done, bf16[2048,1024]{1,0:T(8,128)(2,1)} %bitcast.127), kind=kOutput, calls=%fused_computation.38 | convolution fusion | flops 4296015872 | bytes 10485760 | tf_op jit(solution)/shard_map/dot_general | solution.py:147
  (70 shorter events, 23.5 us)
Async XLA Ops:
  6.5 21.1 %copy-start = (s32[16,2]{0,1:T(2,128)S(1)}, s32[16,2]{0,1:T(2,128)}, u32[]{:S(2)}) copy-start(s32[16,2]{0,1:T(2,128)} %param.12) | copy-start | bytes 388
  6.5 8.2 %copy-start.5 = (bf16[1024,512]{1,0:T(8,128)(2,1)S(1)}, bf16[1024,512]{1,0:T(8,128)(2,1)}, u32[]{:S(2)}) copy-start(bf16[1024,512]{1,0:T(8,128)(2,1)} %param.11) | copy-start | bytes 3145732
  6.5 164.7 %all-gather.6.cloned.1.call-start = ((), (), s32[]{:S(2)}) async-start(), calls=%async_computation.2 | async-start | bytes 2359296 | tf_op jit(solution)/shard_map/all_gather | solution.py:81
  8.1 8.0 %copy-start.3 = (bf16[1024,512]{0,1:T(8,128)(2,1)}, bf16[1024,512]{0,1:T(8,128)(2,1)S(1)}, u32[]{:S(2)}) copy-start(bf16[1024,512]{0,1:T(8,128)(2,1)S(1)} %copy.56) | copy-start | bytes 3145732
  9.0 72.0 %collective-permute-start.7 = (bf16[512,512]{0,1:T(8,128)(2,1)}, bf16[512,512]{0,1:T(8,128)(2,1)}, u32[]{:S(2)}, u32[]{:S(2)}) collective-permute-start(bf16[512,512]{0,1:T(8,128)(2,1)} %slice.16), channel_id=1, source_target_pairs={{0,4},{4,8},{8,12},{12,16},{16,20},{20,24},{24,28},{1,5},{5,9},{9,... | collective-permute-start | bytes 1572872 | tf_op jit(solution)/shard_map/ppermute | solution.py:15
  16.1 69.2 %collective-permute-start.8 = (bf16[512,512]{0,1:T(8,128)(2,1)}, bf16[512,512]{0,1:T(8,128)(2,1)}, u32[]{:S(2)}, u32[]{:S(2)}) collective-permute-start(bf16[512,512]{0,1:T(8,128)(2,1)} %slice.17), channel_id=1, source_target_pairs={{0,4},{4,8},{8,12},{12,16},{16,20},{20,24},{24,28},{1,5},{5,9},{9,... | collective-permute-start | bytes 1572872 | tf_op jit(solution)/shard_map/ppermute | solution.py:15
  23.2 4.6 %copy-start.6 = (f32[8,4]{0,1:T(4,128)S(1)}, f32[8,4]{0,1:T(4,128)}, u32[]{:S(2)}) copy-start(f32[8,4]{0,1:T(4,128)} %param.13) | copy-start | bytes 388
  26.9 3.0 %copy-start.7 = (f32[4]{0:T(128)S(1)}, f32[4]{0:T(128)}, u32[]{:S(2)}) copy-start(f32[4]{0:T(128)} %param.14) | copy-start | bytes 52
  26.9 235.5 %all-gather.4.cloned.1.call-start = ((), (), s32[]{:S(2)}) async-start(), calls=%async_computation.1 | async-start | bytes 5242880 | tf_op jit(solution)/shard_map/all_gather | solution.py:145
  27.0 12.3 %collective-permute-start = (f32[1,4,128]{2,1,0:T(4,128)S(1)}, f32[1,4,128]{2,1,0:T(4,128)S(1)}, u32[]{:S(2)}, u32[]{:S(2)}) collective-permute-start(f32[1,4,128]{2,1,0:T(4,128)S(1)} %bitcast.134), channel_id=1, source_target_pairs={{0,4},{4,8},{8,12},{12,16},{16,20},{20,24},{24,28},{28,0},{1,5},{5... | collective-permute-start | bytes 6152 | tf_op jit(solution)/shard_map/ppermute | solution.py:99
  39.2 7.1 %collective-permute-start.1 = (f32[1,4,128]{2,1,0:T(4,128)S(1)}, f32[1,4,128]{2,1,0:T(4,128)S(1)}, u32[]{:S(2)}, u32[]{:S(2)}) collective-permute-start(f32[1,4,128]{2,1,0:T(4,128)S(1)} %collective-permute-done), channel_id=1, source_target_pairs={{0,4},{4,8},{8,12},{12,16},{16,20},{20,24},{24,28},{28,0},{1,5},{5... | collective-permute-start | bytes 6152 | tf_op jit(solution)/shard_map/ppermute | solution.py:99
  46.3 6.3 %collective-permute-start.2 = (f32[1,4,128]{2,1,0:T(4,128)S(1)}, f32[1,4,128]{2,1,0:T(4,128)S(1)}, u32[]{:S(2)}, u32[]{:S(2)}) collective-permute-start(f32[1,4,128]{2,1,0:T(4,128)S(1)} %collective-permute-done.1), channel_id=1, source_target_pairs={{0,4},{4,8},{8,12},{12,16},{16,20},{20,24},{24,28},{28,0},{1,5},{5... | collective-permute-start | bytes 6152 | tf_op jit(solution)/shard_map/ppermute | solution.py:99
  52.6 6.4 %collective-permute-start.3 = (f32[1,4,128]{2,1,0:T(4,128)S(1)}, f32[1,4,128]{2,1,0:T(4,128)S(1)}, u32[]{:S(2)}, u32[]{:S(2)}) collective-permute-start(f32[1,4,128]{2,1,0:T(4,128)S(1)} %collective-permute-done.2), channel_id=1, source_target_pairs={{0,4},{4,8},{8,12},{12,16},{16,20},{20,24},{24,28},{28,0},{1,5},{5... | collective-permute-start | bytes 6152 | tf_op jit(solution)/shard_map/ppermute | solution.py:99
  59.0 6.5 %collective-permute-start.4 = (f32[1,4,128]{2,1,0:T(4,128)S(1)}, f32[1,4,128]{2,1,0:T(4,128)S(1)}, u32[]{:S(2)}, u32[]{:S(2)}) collective-permute-start(f32[1,4,128]{2,1,0:T(4,128)S(1)} %collective-permute-done.3), channel_id=1, source_target_pairs={{0,4},{4,8},{8,12},{12,16},{16,20},{20,24},{24,28},{28,0},{1,5},{5... | collective-permute-start | bytes 6152 | tf_op jit(solution)/shard_map/ppermute | solution.py:99
  65.5 6.5 %collective-permute-start.5 = (f32[1,4,128]{2,1,0:T(4,128)S(1)}, f32[1,4,128]{2,1,0:T(4,128)S(1)}, u32[]{:S(2)}, u32[]{:S(2)}) collective-permute-start(f32[1,4,128]{2,1,0:T(4,128)S(1)} %collective-permute-done.4), channel_id=1, source_target_pairs={{0,4},{4,8},{8,12},{12,16},{16,20},{20,24},{24,28},{28,0},{1,5},{5... | collective-permute-start | bytes 6152 | tf_op jit(solution)/shard_map/ppermute | solution.py:99
  72.0 6.3 %collective-permute-start.6 = (f32[1,4,128]{2,1,0:T(4,128)S(1)}, f32[1,4,128]{2,1,0:T(4,128)S(1)}, u32[]{:S(2)}, u32[]{:S(2)}) collective-permute-start(f32[1,4,128]{2,1,0:T(4,128)S(1)} %collective-permute-done.5), channel_id=1, source_target_pairs={{0,4},{4,8},{8,12},{12,16},{16,20},{20,24},{24,28},{28,0},{1,5},{5... | collective-permute-start | bytes 6152 | tf_op jit(solution)/shard_map/ppermute | solution.py:99
  73.8 7.2 %copy-start.4 = (bf16[1024,512]{0,1:T(8,128)(2,1)S(1)}, bf16[1024,512]{0,1:T(8,128)(2,1)}, u32[]{:S(2)}) copy-start(bf16[1024,512]{0,1:T(8,128)(2,1)} %copy-done.3) | copy-start | bytes 3145732
  171.3 4.6 %copy-start.2 = (f32[1024,512]{0,1:T(8,128)S(1)}, f32[1024,512]{0,1:T(8,128)}, u32[]{:S(2)}) copy-start(f32[1024,512]{0,1:T(8,128)} %copy.78) | copy-start | bytes 6291460
  262.4 9.4 %copy-start.1 = (s32[16,2]{0,1:T(2,128)S(1)}, s32[16,2]{0,1:T(2,128)}, u32[]{:S(2)}) copy-start(s32[16,2]{0,1:T(2,128)} %param.12) | copy-start | bytes 388
Sparse Core Ops, SparseCore 0:
  27.0 49.7 all-gather.5
  180.8 46.7 all-gather.3
